TPU v7x, 32 devices: a whole 2x2x4 slice. The times are simulated.
32 devices in a mesh: seq: 16 (over z, x, core), tp: 2 (over y).
Axes of the slice: x: 2, y: 2, z: 4, core: 2. Of those that a mesh axis runs over, the one named last changes fastest.
Arguments:
- hidden_in: bfloat16 [2048, 4096], P('seq', 'tp'), may hold values from -64 to 64
- span_order: int32 [16], replicated, may hold values from 0 to 15, each once
- norm_gain: bfloat16 [4096], P('tp'), may hold values from 0.099609375 to 1.8984375
- w_query: bfloat16 [4096, 4096], P('seq', 'tp'), may hold values from -0.09375 to 0.09375
- bias_query: bfloat16 [4096], P('tp'), may hold values from -14 to 14
- key_value_weight: bfloat16 [4096, 2, 1024], P('seq', None, 'tp'), may hold values from -0.09375 to 0.09375
- bias_kv: bfloat16 [2, 1024], P(None, 'tp'), may hold values from -14 to 14
- w_out: bfloat16 [4096, 4096], P('tp', 'seq'), may hold values from -0.09375 to 0.09375
- post_gain: bfloat16 [4096], P('tp'), may hold values from 0.099609375 to 1.8984375
Outputs:
- attn_out: bfloat16 [2048, 4096], P('seq', 'tp')
- normed: bfloat16 [2048, 4096], P('seq', 'tp')
Inputs may be any that keep to these rules, and one draw needn't show every extreme that they name: Each span number appears once; row r of hidden_in belongs to span span_order[r // 128].
All inputs are finite; a program needn't handle non-finite values.
Results may differ from a plain program's by a relative error of at most 0.014.
Values may be sent and summed in bfloat16 or wider, within the bound.
A program may use at most 128 MiB of HBM per device.

v0:
```python
import math
import jax
import jax.numpy as jnp
from jax import lax
from jax.sharding import PartitionSpec as P

MODEL_WIDTH = 4096
HEAD_SIZE = 128
GROUP = 4
eps = 1e-06
rope_base = 1000000.0


def apply_rotary(field, token_positions):
    half = field.shape[-1] // 2
    inverse = jnp.exp(-math.log(rope_base) * jnp.arange(half, dtype=jnp.float32) / half)
    angles = token_positions.astype(jnp.float32)[:, None] * inverse[None, :]
    cosine = jnp.cos(angles)[:, None, :]
    sine = jnp.sin(angles)[:, None, :]
    first = field[..., :half]
    second = field[..., half:]
    return jnp.concatenate(
        [first * cosine - second * sine, second * cosine + first * sine], axis=-1
    )


def span_lookup(order, devices):
    table_ids = jnp.arange(order.shape[0], dtype=jnp.int32)
    return jnp.sum(jnp.where(devices[:, None] == table_ids[None, :], order[None, :], 0), axis=1)


def per_device(
    hidden_in,
    span_order,
    norm_gain,
    w_query,
    bias_query,
    key_value_weight,
    bias_kv,
    w_out,
    post_gain,
):
    tok_rows = hidden_in.shape[0]
    seq_index = lax.axis_index("seq")
    own_span = span_lookup(span_order, jnp.full((1,), seq_index, jnp.int32))[0]
    token_positions = own_span * tok_rows + jnp.arange(tok_rows, dtype=jnp.int32)
    local = hidden_in.astype(jnp.float32)
    raw_rows, gains = (
        lax.all_gather(hidden_in, "tp", axis=1, tiled=True),
        lax.all_gather(norm_gain[None, :], "tp", axis=1, tiled=True),
    )
    full_rows = raw_rows.astype(jnp.float32)
    meansq = jnp.mean(full_rows * full_rows, axis=1, keepdims=True)
    normed_in = (full_rows * lax.rsqrt(meansq + eps) * gains.astype(jnp.float32)).astype(
        jnp.bfloat16
    )
    columns = normed_in
    query_proj = jnp.dot(
        columns,
        lax.all_gather(w_query, "seq", axis=0, tiled=True),
        preferred_element_type=jnp.float32,
    )
    columns = normed_in
    pair_proj = jnp.einsum(
        "tr,rkc->tkc",
        columns,
        lax.all_gather(key_value_weight, "seq", axis=0, tiled=True),
        preferred_element_type=jnp.float32,
    )
    query_heads = w_query.shape[1] // HEAD_SIZE
    kv_heads = key_value_weight.shape[2] // HEAD_SIZE
    query_proj = query_proj + bias_query.astype(jnp.float32)[None, :]
    queries = apply_rotary(
        query_proj.reshape(tok_rows, query_heads, HEAD_SIZE), token_positions
    ).astype(jnp.bfloat16)
    pair_proj = pair_proj + bias_kv.astype(jnp.float32)[None, :, :]
    rotated_keys = apply_rotary(
        pair_proj[:, 0, :].reshape(tok_rows, kv_heads, HEAD_SIZE), token_positions
    )
    rotated_keys = rotated_keys.astype(jnp.bfloat16).reshape(tok_rows, kv_heads * HEAD_SIZE)
    value_rows = pair_proj[:, 1, :].astype(jnp.bfloat16)
    grouped = (
        queries.reshape(tok_rows, kv_heads, GROUP, HEAD_SIZE)
        .transpose(1, 2, 0, 3)
        .reshape(kv_heads, GROUP * tok_rows, HEAD_SIZE)
    )
    query_pos = jnp.tile(token_positions, GROUP)
    last_query = jnp.max(token_positions)
    scale = 1.0 / math.sqrt(HEAD_SIZE)
    start_state = (
        jnp.full((kv_heads, GROUP * tok_rows), -1e30, jnp.float32),
        jnp.zeros((kv_heads, GROUP * tok_rows), jnp.float32),
        jnp.zeros((kv_heads, GROUP * tok_rows, HEAD_SIZE), jnp.float32),
    )
    key_piece = lax.all_gather(rotated_keys, "seq", axis=0, tiled=True)
    value_piece = lax.all_gather(value_rows, "seq", axis=0, tiled=True)
    count = key_piece.shape[0]
    block = math.gcd(count, 1536)

    def visit(step, state):
        first = step * block
        key_block = lax.dynamic_slice_in_dim(key_piece, first, block, 0).reshape(
            block, kv_heads, HEAD_SIZE
        )
        value_block = lax.dynamic_slice_in_dim(value_piece, first, block, 0).reshape(
            block, kv_heads, HEAD_SIZE
        )
        row_ids = first + jnp.arange(block, dtype=jnp.int32)
        key_pos = span_lookup(span_order, row_ids // tok_rows) * tok_rows + row_ids % tok_rows

        def update(current):
            maxima, totals, sums = current
            scores = (
                jnp.einsum("kqd,nkd->kqn", grouped, key_block, preferred_element_type=jnp.float32)
                * scale
            )
            allowed = (key_pos[None, :] <= query_pos[:, None])[None, :, :]
            scores = jnp.where(allowed, scores, -1e30)
            fresh = jnp.maximum(maxima, jnp.max(scores, axis=2))
            weights = jnp.where(allowed, jnp.exp(scores - fresh[:, :, None]), 0.0)
            factor = jnp.exp(maxima - fresh)
            totals = totals * factor + jnp.sum(weights, axis=2)
            sums = sums * factor[:, :, None] + jnp.einsum(
                "kqn,nkd->kqd",
                weights.astype(jnp.bfloat16),
                value_block,
                preferred_element_type=jnp.float32,
            )
            return (fresh, totals, sums)

        return lax.cond(jnp.min(key_pos) <= last_query, update, lambda current: current, state)

    maxima, totals, sums = lax.fori_loop(0, count // block, visit, start_state)
    attended = (sums / totals[:, :, None]).astype(jnp.bfloat16)
    attended = (
        attended.reshape(kv_heads, GROUP, tok_rows, HEAD_SIZE)
        .transpose(2, 0, 1, 3)
        .reshape(tok_rows, query_heads * HEAD_SIZE)
    )
    partial_out = jnp.dot(
        attended,
        lax.all_gather(w_out, "seq", axis=1, tiled=True),
        preferred_element_type=jnp.float32,
    )
    mixed = lax.psum_scatter(
        partial_out.astype(jnp.bfloat16), "tp", scatter_dimension=1, tiled=True
    ).astype(jnp.float32)
    attn_out = mixed.astype(jnp.bfloat16)
    stream = local + mixed
    post_sq = lax.psum(jnp.sum(stream * stream, axis=1), "tp")
    normed = (
        stream
        * lax.rsqrt(post_sq / MODEL_WIDTH + eps)[:, None]
        * post_gain.astype(jnp.float32)[None, :]
    ).astype(jnp.bfloat16)
    return (attn_out, normed)


def solution(mesh):
    placed = (
        P("seq", "tp"),
        P(),
        P("tp"),
        P("seq", "tp"),
        P("tp"),
        P("seq", None, "tp"),
        P(None, "tp"),
        P("tp", "seq"),
        P("tp"),
    )
    return jax.shard_map(
        per_device,
        mesh=mesh,
        in_specs=placed,
        out_specs=(P("seq", "tp"), P("seq", "tp")),
        check_vma=False,
    )
```

profile of v0, /device:TPU:0, one launch (start us, length us, event | category | flops | bytes accessed | tf_op | source)
XLA Modules:
  0.0 499.7 jit_solution(17849845767442077635)
XLA Ops:
  7.9 1.9 copy.44
  9.9 5.5 %all-gather = bf16[4096]{0:T(1024)(128)(2,1)S(1)} all-gather(bf16[2048]{0:T(1024)(128)(2,1)} %param.15), channel_id=2, replica_groups=mesh['seq'=16,'tp'=2] {'tp'}, dimensions={0}, use_global_device_ids=true | all-gather | bytes 12288 | tf_op jit(solution)/shard_map/all_gather | solution.py:50
  16.1 17.4 %all-gather.9.cloned.1.call-done = bf16[128,4096]{1,0:T(8,128)(2,1)} async-done(((bf16[128,2048]{1,0:T(8,128)(2,1)}), bf16[128,4096]{1,0:T(8,128)(2,1)}) %all-gather.9.cloned.1.call-update) | async-done | bytes 1048592 | tf_op jit(solution)/shard_map/all_gather | solution.py:49
  35.1 75.6 %all-gather.11.cloned.1.call-done = bf16[4096,2,512]{2,0,1:T(8,128)(2,1)} async-done(((bf16[256,2,512]{2,0,1:T(8,128)(2,1)}), bf16[4096,2,512]{2,0,1:T(8,128)(2,1)}) %all-gather.11.cloned.1.call-update) | async-done | bytes 8388624 | tf_op jit(solution)/shard_map/all_gather | solution.py:67
  110.7 5.0 %convolution_add_fusion.1 = f32[128,2,512]{2,0,1:T(8,128)S(1)} fusion(bf16[4096,2,512]{2,0,1:T(8,128)(2,1)} %all-gather.11.cloned.1.call-done, bf16[128,4096]{1,0:T(8,128)(2,1)} %all-gather.9.cloned.1.call-done, f32[4096]{0:T(1024)S(1)} %mul.210, f32[128]{0:T(128)S(1)} %add_rsqrt_fusion.1, f32[2,512]{1,0:T(2,128)S(1)} %convert_element_type.69), kind=kOutput, calls=%fused_computation.39 | convolution fusion | flops 1075970048 | bytes 9982464 | tf_op jit(solution)/shard_map/tr,rkc->tkc/dot_general | solution.py:64
  121.5 35.1 %all-gather.19.cloned.1.call-done = bf16[2048,1,512]{2,0,1:T(8,128)(2,1)} async-done(((bf16[128,1,512]{2,0,1:T(8,128)(2,1)}), bf16[2048,1,512]{2,0,1:T(8,128)(2,1)}) %all-gather.19.cloned.1.call-update) | async-done | bytes 2097168 | tf_op jit(solution)/shard_map/all_gather | solution.py:96
  156.6 2.9 copy.48
  159.5 124.3 %all-gather.15.cloned.1.call-done = bf16[4096,2048]{1,0:T(8,128)(2,1)} async-done(((bf16[256,2048]{1,0:T(8,128)(2,1)}), bf16[4096,2048]{1,0:T(8,128)(2,1)}) %all-gather.15.cloned.1.call-update) | async-done | bytes 16777232 | tf_op jit(solution)/shard_map/all_gather | solution.py:60
  283.8 8.2 %fusion.21 = f32[16,8,16,128]{3,1,2,0:T(8,128)S(1)} fusion(bf16[4096,2048]{1,0:T(8,128)(2,1)} %all-gather.15.cloned.1.call-done, f32[2048]{0:T(1024)S(1)} %convert_element_type.72, bf16[128,4096]{1,0:T(8,128)(2,1)S(1)} %copy-done, f32[4096]{0:T(1024)S(1)} %mul.210, f32[128]{0:T(128)S(1)} %add_rsqrt_fusion.1), kind=kOutput, calls=%fused_computation.38 | convolution fusion | flops 2149842944 | bytes 18899456 | tf_op jit(solution)/shard_map/dot_general | solution.py:58
  293.3 32.3 %all-gather.13.cloned.1.call-done = bf16[2048,512]{0,1:T(8,128)(2,1)} async-done(((bf16[128,512]{0,1:T(8,128)(2,1)}), bf16[2048,512]{0,1:T(8,128)(2,1)}) %all-gather.13.cloned.1.call-update) | async-done | bytes 2097168 | tf_op jit(solution)/shard_map/all_gather | solution.py:95
  326.7 33.3 %while.20 = (s32[]{:T(128)}, f32[4,512]{1,0:T(4,128)S(1)}, f32[4,512]{1,0:T(4,128)S(1)}, f32[4,512,128]{2,1,0:T(8,128)}, s32[16]{0:T(128)S(1)}, /*index=5*/s32[]...) while((s32[]{:T(128)}, f32[4,512]{1,0:T(4,128)S(1)}, ...), condition=%wide.region_10.11_spmd.clone, body=%wide.region_3.10_spmd.clone.sunk | while | flops 551332864 | bytes 27935672 | solution.py:133
  328.7 6.3 %conditional.3 = ((f32[4,512]{1,0:T(4,128)S(1)}, f32[4,512]{1,0:T(4,128)S(1)}, f32[4,512,128]{2,1,0:T(8,128)})) conditional(s32[]{:T(128)} %convert_element_type.117, (f32[4,512]{1,0:T(4,128)S(1)}, f32[4,512]{1,0:T(4,128)S(1)}, f32[4,512,128]{2,1,0:T(8,128)}) %tuple.77, (s32[512]{0:T(512)S(1)}, s32[128]{0:T(128)S(1)}, s32[]{:T(128)}, ...), branch_computations={%region_6.6_spmd, %region_7.9_spmd} | conditional | flops 551292928 | bytes 27925118 | solution.py:131
  332.2 1.8 fusion.8
  337.0 6.3 %conditional.3 = ((f32[4,512]{1,0:T(4,128)S(1)}, f32[4,512]{1,0:T(4,128)S(1)}, f32[4,512,128]{2,1,0:T(8,128)})) conditional(s32[]{:T(128)} %convert_element_type.117, (f32[4,512]{1,0:T(4,128)S(1)}, f32[4,512]{1,0:T(4,128)S(1)}, f32[4,512,128]{2,1,0:T(8,128)}) %tuple.77, (s32[512]{0:T(512)S(1)}, s32[128]{0:T(128)S(1)}, s32[]{:T(128)}, ...), branch_computations={%region_6.6_spmd, %region_7.9_spmd} | conditional | flops 551292928 | bytes 27925118 | solution.py:131
  340.6 1.8 fusion.8
  345.4 6.3 %conditional.3 = ((f32[4,512]{1,0:T(4,128)S(1)}, f32[4,512]{1,0:T(4,128)S(1)}, f32[4,512,128]{2,1,0:T(8,128)})) conditional(s32[]{:T(128)} %convert_element_type.117, (f32[4,512]{1,0:T(4,128)S(1)}, f32[4,512]{1,0:T(4,128)S(1)}, f32[4,512,128]{2,1,0:T(8,128)}) %tuple.77, (s32[512]{0:T(512)S(1)}, s32[128]{0:T(128)S(1)}, s32[]{:T(128)}, ...), branch_computations={%region_6.6_spmd, %region_7.9_spmd} | conditional | flops 551292928 | bytes 27925118 | solution.py:131
  348.9 1.8 fusion.8
  353.7 6.3 %conditional.3 = ((f32[4,512]{1,0:T(4,128)S(1)}, f32[4,512]{1,0:T(4,128)S(1)}, f32[4,512,128]{2,1,0:T(8,128)})) conditional(s32[]{:T(128)} %convert_element_type.117, (f32[4,512]{1,0:T(4,128)S(1)}, f32[4,512]{1,0:T(4,128)S(1)}, f32[4,512,128]{2,1,0:T(8,128)}) %tuple.77, (s32[512]{0:T(512)S(1)}, s32[128]{0:T(128)S(1)}, s32[]{:T(128)}, ...), branch_computations={%region_6.6_spmd, %region_7.9_spmd} | conditional | flops 551292928 | bytes 27925118 | solution.py:131
  357.2 1.8 fusion.8
  361.8 94.8 %all-gather.17.cloned.1.call-done = bf16[2048,4096]{1,0:T(8,128)(2,1)} async-done(((bf16[2048,256]{1,0:T(8,128)(2,1)}), bf16[2048,4096]{1,0:T(8,128)(2,1)}) %all-gather.17.cloned.1.call-update) | async-done | bytes 16777232 | tf_op jit(solution)/shard_map/all_gather | solution.py:142
  456.6 9.2 %convolution_convert_fusion = bf16[128,4096]{1,0:T(8,128)(2,1)} fusion(bf16[128,2048]{0,1:T(8,128)(2,1)S(1)} %bitcast.47, bf16[2048,4096]{1,0:T(8,128)(2,1)} %all-gather.17.cloned.1.call-done), kind=kOutput, calls=%fused_computation.31 | convolution fusion | flops 2148007936 | bytes 18350080 | tf_op jit(solution)/shard_map/dot_general | solution.py:140
  465.9 18.7 %reduce-scatter.2.cloned.1.call-done = bf16[128,2048]{1,0:T(8,128)(2,1)} async-done(((bf16[128,4096]{1,0:T(8,128)(2,1)}), bf16[128,2048]{1,0:T(8,128)(2,1)}) %reduce-scatter.2.cloned.1.call-update) | async-done | bytes 524304 | tf_op jit(solution)/shard_map/reduce_scatter | solution.py:145
  485.9 4.9 psum.7
  490.8 2.0 multiply_convert_fusion
  (113 shorter events, 34.3 us)
Async XLA Ops:
  7.2 26.4 %all-gather.9.cloned.1.call-start = ((), (), s32[]{:S(2)}) async-start(), calls=%async_computation.1 | async-start | bytes 1572864 | tf_op jit(solution)/shard_map/all_gather | solution.py:49
  7.9 102.8 %all-gather.11.cloned.1.call-start = ((), (), s32[]{:S(2)}) async-start(), calls=%async_computation.2 | async-start | bytes 8912896 | tf_op jit(solution)/shard_map/all_gather | solution.py:67
  9.9 146.8 %all-gather.19.cloned.1.call-start = ((), (), s32[]{:S(2)}) async-start(), calls=%async_computation.7 | async-start | bytes 2228224 | tf_op jit(solution)/shard_map/all_gather | solution.py:96
  35.1 81.9 %copy-start.4 = (s32[16]{0:T(128)S(1)}, s32[16]{0:T(128)}, u32[]{:S(2)}) copy-start(s32[16]{0:T(128)} %param.14) | copy-start | bytes 196
  115.7 5.2 %copy-start.5 = (bf16[2048]{0:T(1024)(128)(2,1)S(1)}, bf16[2048]{0:T(1024)(128)(2,1)}, u32[]{:S(2)}) copy-start(bf16[2048]{0:T(1024)(128)(2,1)} %param.17) | copy-start | bytes 12292
  116.4 167.4 %all-gather.15.cloned.1.call-start = ((), (), s32[]{:S(2)}) async-start(), calls=%async_computation.4 | async-start | bytes 17825792 | tf_op jit(solution)/shard_map/all_gather | solution.py:60
  117.0 166.8 %copy-start = (bf16[128,4096]{1,0:T(8,128)(2,1)S(1)}, bf16[128,4096]{1,0:T(8,128)(2,1)}, u32[]{:S(2)}) copy-start(bf16[128,4096]{1,0:T(8,128)(2,1)} %all-gather.9.cloned.1.call-done) | copy-start | bytes 3145732
  117.0 208.7 %all-gather.13.cloned.1.call-start = ((), (), s32[]{:S(2)}) async-start(), calls=%async_computation.3 | async-start | bytes 2228224 | tf_op jit(solution)/shard_map/all_gather | solution.py:95
  120.1 336.6 %all-gather.17.cloned.1.call-start = ((), (), s32[]{:S(2)}) async-start(), calls=%async_computation.5 | async-start | bytes 17825792 | tf_op jit(solution)/shard_map/all_gather | solution.py:142
  120.7 363.9 %reduce-scatter.2.cloned.1.call-start = ((), (), s32[]{:S(2)}) async-start(), calls=%async_computation.6 | async-start | bytes 1572864 | tf_op jit(solution)/shard_map/reduce_scatter | solution.py:145
  330.1 2.1 copy-start.2
  334.0 1.0 copy-start.3
  338.4 2.1 copy-start.2
  342.4 1.0 copy-start.3
  346.8 2.1 copy-start.2
  350.7 1.0 copy-start.3
  355.1 2.1 copy-start.2
  359.0 1.0 copy-start.3
  456.6 9.2 %copy-start.6 = (bf16[2048]{0:T(1024)(128)(2,1)S(1)}, bf16[2048]{0:T(1024)(128)(2,1)}, u32[]{:S(2)}) copy-start(bf16[2048]{0:T(1024)(128)(2,1)} %param.21) | copy-start | bytes 12292
  456.6 27.9 %copy-start.1 = (bf16[128,2048]{1,0:T(8,128)(2,1)S(1)}, bf16[128,2048]{1,0:T(8,128)(2,1)}, u32[]{:S(2)}) copy-start(bf16[128,2048]{1,0:T(8,128)(2,1)} %param.13) | copy-start | bytes 1572868
Sparse Core Ops, SparseCore 0:
  9.5 23.9 all-gather.8
  36.3 74.2 all-gather.10
  116.5 40.0 all-gather.18
  158.6 125.1 all-gather.14
  286.4 39.2 all-gather.12
  327.7 128.9 all-gather.16
  466.0 18.5 reduce-scatter.1
where the time goes:
time: 500 us
  waiting for transfers between devices  400 us (80%)
  matrix products  33.6 us (7%)
  other arithmetic  18.1 us (4%)
  local copies, waits for them, and re-layouts  16.7 us (3%)
  between operations  15 us (3%)
  blocking collectives  10.4 us (2%)
  loops' own time  5.46 us (1%)
    all_gather x1, waiting for transfers between devices, per_device(): lax.all_gather(w_query, 'seq', axis=0, tiled=True)  124 us
    all_gather x1, waiting for transfers between devices, per_device(): lax.all_gather(w_out, 'seq', axis=1, tiled=True)  94.8 us
    all_gather x1, waiting for transfers between devices, per_device(): lax.all_gather(key_value_weight, 'seq', axis=0, tiled=True)  75.6 us
    all_gather x1, waiting for transfers between devices, per_device(): value_piece = lax.all_gather(value_rows, 'seq', axis=0, tiled=True)  35.1 us
    all_gather x1, waiting for transfers between devices, per_device(): key_piece = lax.all_gather(rotated_keys, 'seq', axis=0, tiled=True)  32.3 us
    reduce_scatter x1, waiting for transfers between devices, per_device(): lax.psum_scatter(partial_out.astype(jnp.bfloat16), 'tp', scatter_dimensio...  18.7 us
    all_gather x1, waiting for transfers between devices, per_device(): lax.all_gather(hidden_in, 'tp', axis=1, tiled=True)  17.4 us
  transfers between devices with their start and end apart: 7, of which 7 were waited for; matrix products, arithmetic and copies ran while one was open for 9% of the time, Pallas kernels for 0%

commit v1 on v0

--- a/solution.py
+++ b/solution.py
@@ -92,7 +92,12 @@
         jnp.zeros((kv_heads, GROUP * tok_rows), jnp.float32),
         jnp.zeros((kv_heads, GROUP * tok_rows, HEAD_SIZE), jnp.float32),
     )
-    key_piece = lax.all_gather(rotated_keys, "seq", axis=0, tiled=True)
+    ring = [rotated_keys]
+    for hop in range(15):
+        ring.append(lax.ppermute(ring[-1], "seq", [(dev, (dev + 1) % 16) for dev in range(16)]))
+    key_piece = jnp.roll(
+        jnp.concatenate(ring[::-1], axis=0), (lax.axis_index("seq") + 1) * ring[0].shape[0], axis=0
+    )
     value_piece = lax.all_gather(value_rows, "seq", axis=0, tiled=True)
     count = key_piece.shape[0]
     block = math.gcd(count, 1536)

time: 500 us -> 469 us (0.938)
  waiting for transfers between devices: 400 us -> 366 us
    ppermute x0 -> x15, waiting for transfers between devices: none -> 129 us  [per_device(): lax.ppermute(ring[-1], 'seq', [(dev, (dev + 1) % 16) for dev in range(16)])]
    all_gather x1, waiting for transfers between devices: 124 us -> 37.6 us  [per_device(): lax.all_gather(w_query, 'seq', axis=0, tiled=True)]
    all_gather x1, waiting for transfers between devices: 35.1 us -> 0.02 us  [per_device(): value_piece = lax.all_gather(value_rows, 'seq', axis=0, tiled=True)]
    all_gather x1 -> x0, waiting for transfers between devices: 32.3 us -> none  [per_device(): key_piece = lax.all_gather(rotated_keys, 'seq', axis=0, tiled=True)]
    all_gather x1, waiting for transfers between devices: 94.8 us -> 85.9 us  [per_device(): lax.all_gather(w_out, 'seq', axis=1, tiled=True)]
  transfers between devices with their start and end apart: 7 -> 21, of which waited for: 7 -> 20; matrix products, arithmetic and copies ran while one was open for 9% -> 10% of each run, Pallas kernels for 0% -> 0%
where the time goes in v1:
time: 469 us; the launch traced here: 468 us
  waiting for transfers between devices  366 us (78%)
  matrix products  33.6 us (7%)
  local copies, waits for them, and re-layouts  18.7 us (4%)
  other arithmetic  18.2 us (4%)
  between operations  15.2 us (3%)
  blocking collectives  10.4 us (2%)
  loops' own time  5.43 us (1%)
    ppermute x15, waiting for transfers between devices, per_device(): lax.ppermute(ring[-1], 'seq', [(dev, (dev + 1) % 16) for dev in range(16)])  129 us
    all_gather x1, waiting for transfers between devices, per_device(): lax.all_gather(w_out, 'seq', axis=1, tiled=True)  85.9 us
    all_gather x1, waiting for transfers between devices, per_device(): lax.all_gather(key_value_weight, 'seq', axis=0, tiled=True)  75.6 us
    all_gather x1, waiting for transfers between devices, per_device(): lax.all_gather(w_query, 'seq', axis=0, tiled=True)  37.6 us
    reduce_scatter x1, waiting for transfers between devices, per_device(): lax.psum_scatter(partial_out.astype(jnp.bfloat16), 'tp', scatter_dimensio...  18.7 us
    all_gather x1, waiting for transfers between devices, per_device(): lax.all_gather(hidden_in, 'tp', axis=1, tiled=True)  17.4 us
  transfers between devices with their start and end apart: 21, of which 20 were waited for; matrix products, arithmetic and copies ran while one was open for 10% of the time, Pallas kernels for 0%

profile of v1, /device:TPU:0, one launch (start us, length us, event | category | flops | bytes accessed | tf_op | source)
XLA Modules:
  0.0 467.9 jit_solution(12692073814429591210)
XLA Ops:
  16.1 17.4 %all-gather.8.cloned.1.call-done = bf16[128,4096]{1,0:T(8,128)(2,1)} async-done(((bf16[128,2048]{1,0:T(8,128)(2,1)}), bf16[128,4096]{1,0:T(8,128)(2,1)}) %all-gather.8.cloned.1.call-update) | async-done | bytes 1048592 | tf_op jit(solution)/shard_map/all_gather | solution.py:49
  35.1 75.6 %all-gather.10.cloned.1.call-done = bf16[4096,2,512]{2,0,1:T(8,128)(2,1)} async-done(((bf16[256,2,512]{2,0,1:T(8,128)(2,1)}), bf16[4096,2,512]{2,0,1:T(8,128)(2,1)}) %all-gather.10.cloned.1.call-update) | async-done | bytes 8388624 | tf_op jit(solution)/shard_map/all_gather | solution.py:67
  120.3 7.0 %collective-permute-done = bf16[128,512]{0,1:T(8,128)(2,1)S(1)} collective-permute-done((bf16[128,512]{0,1:T(8,128)(2,1)S(1)}, bf16[128,512]{0,1:T(8,128)(2,1)S(1)}, u32[]{:S(2)}, u32[]{:S(2)}) %collective-permute-start) | collective-permute-done | bytes 131104 | tf_op jit(solution)/shard_map/ppermute | solution.py:97
  127.3 8.0 %collective-permute-done.1 = bf16[128,512]{0,1:T(8,128)(2,1)S(1)} collective-permute-done((bf16[128,512]{0,1:T(8,128)(2,1)S(1)}, bf16[128,512]{0,1:T(8,128)(2,1)S(1)}, u32[]{:S(2)}, u32[]{:S(2)}) %collective-permute-start.1) | collective-permute-done | bytes 131104 | tf_op jit(solution)/shard_map/ppermute | solution.py:97
  135.2 7.1 %collective-permute-done.2 = bf16[128,512]{0,1:T(8,128)(2,1)S(1)} collective-permute-done((bf16[128,512]{0,1:T(8,128)(2,1)S(1)}, bf16[128,512]{0,1:T(8,128)(2,1)S(1)}, u32[]{:S(2)}, u32[]{:S(2)}) %collective-permute-start.2) | collective-permute-done | bytes 131104 | tf_op jit(solution)/shard_map/ppermute | solution.py:97
  142.3 8.5 %collective-permute-done.3 = bf16[128,512]{0,1:T(8,128)(2,1)S(1)} collective-permute-done((bf16[128,512]{0,1:T(8,128)(2,1)S(1)}, bf16[128,512]{0,1:T(8,128)(2,1)S(1)}, u32[]{:S(2)}, u32[]{:S(2)}) %collective-permute-start.3) | collective-permute-done | bytes 131104 | tf_op jit(solution)/shard_map/ppermute | solution.py:97
  150.8 7.3 %collective-permute-done.4 = bf16[128,512]{0,1:T(8,128)(2,1)S(1)} collective-permute-done((bf16[128,512]{0,1:T(8,128)(2,1)S(1)}, bf16[128,512]{0,1:T(8,128)(2,1)S(1)}, u32[]{:S(2)}, u32[]{:S(2)}) %collective-permute-start.4) | collective-permute-done | bytes 131104 | tf_op jit(solution)/shard_map/ppermute | solution.py:97
  158.1 7.1 %collective-permute-done.5 = bf16[128,512]{0,1:T(8,128)(2,1)S(1)} collective-permute-done((bf16[128,512]{0,1:T(8,128)(2,1)S(1)}, bf16[128,512]{0,1:T(8,128)(2,1)S(1)}, u32[]{:S(2)}, u32[]{:S(2)}) %collective-permute-start.5) | collective-permute-done | bytes 131104 | tf_op jit(solution)/shard_map/ppermute | solution.py:97
  165.2 7.2 %collective-permute-done.6 = bf16[128,512]{0,1:T(8,128)(2,1)S(1)} collective-permute-done((bf16[128,512]{0,1:T(8,128)(2,1)S(1)}, bf16[128,512]{0,1:T(8,128)(2,1)S(1)}, u32[]{:S(2)}, u32[]{:S(2)}) %collective-permute-start.6) | collective-permute-done | bytes 131104 | tf_op jit(solution)/shard_map/ppermute | solution.py:97
  172.4 10.0 %collective-permute-done.7 = bf16[128,512]{0,1:T(8,128)(2,1)S(1)} collective-permute-done((bf16[128,512]{0,1:T(8,128)(2,1)S(1)}, bf16[128,512]{0,1:T(8,128)(2,1)S(1)}, u32[]{:S(2)}, u32[]{:S(2)}) %collective-permute-start.7) | collective-permute-done | bytes 131104 | tf_op jit(solution)/shard_map/ppermute | solution.py:97
  182.4 10.0 %collective-permute-done.8 = bf16[128,512]{0,1:T(8,128)(2,1)S(1)} collective-permute-done((bf16[128,512]{0,1:T(8,128)(2,1)S(1)}, bf16[128,512]{0,1:T(8,128)(2,1)S(1)}, u32[]{:S(2)}, u32[]{:S(2)}) %collective-permute-start.8) | collective-permute-done | bytes 131104 | tf_op jit(solution)/shard_map/ppermute | solution.py:97
  192.5 10.0 %collective-permute-done.9 = bf16[128,512]{0,1:T(8,128)(2,1)S(1)} collective-permute-done((bf16[128,512]{0,1:T(8,128)(2,1)S(1)}, bf16[128,512]{0,1:T(8,128)(2,1)S(1)}, u32[]{:S(2)}, u32[]{:S(2)}) %collective-permute-start.9) | collective-permute-done | bytes 131104 | tf_op jit(solution)/shard_map/ppermute | solution.py:97
  202.5 10.0 %collective-permute-done.10 = bf16[128,512]{0,1:T(8,128)(2,1)S(1)} collective-permute-done((bf16[128,512]{0,1:T(8,128)(2,1)S(1)}, bf16[128,512]{0,1:T(8,128)(2,1)S(1)}, u32[]{:S(2)}, u32[]{:S(2)}) %collective-permute-start.10) | collective-permute-done | bytes 131104 | tf_op jit(solution)/shard_map/ppermute | solution.py:97
  212.5 7.2 %collective-permute-done.11 = bf16[128,512]{0,1:T(8,128)(2,1)S(1)} collective-permute-done((bf16[128,512]{0,1:T(8,128)(2,1)S(1)}, bf16[128,512]{0,1:T(8,128)(2,1)S(1)}, u32[]{:S(2)}, u32[]{:S(2)}) %collective-permute-start.11) | collective-permute-done | bytes 131104 | tf_op jit(solution)/shard_map/ppermute | solution.py:97
  219.6 10.0 %collective-permute-done.12 = bf16[128,512]{0,1:T(8,128)(2,1)S(1)} collective-permute-done((bf16[128,512]{0,1:T(8,128)(2,1)S(1)}, bf16[128,512]{0,1:T(8,128)(2,1)S(1)}, u32[]{:S(2)}, u32[]{:S(2)}) %collective-permute-start.12) | collective-permute-done | bytes 131104 | tf_op jit(solution)/shard_map/ppermute | solution.py:97
  229.7 10.0 %collective-permute-done.13 = bf16[128,512]{0,1:T(8,128)(2,1)S(1)} collective-permute-done((bf16[128,512]{0,1:T(8,128)(2,1)S(1)}, bf16[128,512]{0,1:T(8,128)(2,1)S(1)}, u32[]{:S(2)}, u32[]{:S(2)}) %collective-permute-start.13) | collective-permute-done | bytes 131104 | tf_op jit(solution)/shard_map/ppermute | solution.py:97
  240.4 9.4 %collective-permute-done.14 = bf16[128,512]{0,1:T(8,128)(2,1)S(1)} collective-permute-done((bf16[128,512]{0,1:T(8,128)(2,1)S(1)}, bf16[128,512]{0,1:T(8,128)(2,1)S(1)}, u32[]{:S(2)}, u32[]{:S(2)}) %collective-permute-start.14) | collective-permute-done | bytes 131104 | tf_op jit(solution)/shard_map/ppermute | solution.py:97
  255.5 37.6 %all-gather.12.cloned.1.call-done = bf16[4096,2048]{1,0:T(8,128)(2,1)} async-done(((bf16[256,2048]{1,0:T(8,128)(2,1)}), bf16[4096,2048]{1,0:T(8,128)(2,1)}) %all-gather.12.cloned.1.call-update) | async-done | bytes 16777232 | tf_op jit(solution)/shard_map/all_gather | solution.py:60
  293.2 8.2 %fusion.21 = f32[16,8,16,128]{3,1,2,0:T(8,128)S(1)} fusion(bf16[4096,2048]{1,0:T(8,128)(2,1)} %all-gather.12.cloned.1.call-done, f32[2048]{0:T(1024)S(1)} %convert_element_type.72, bf16[128,4096]{1,0:T(8,128)(2,1)S(1)} %copy-done, f32[4096]{0:T(1024)S(1)} %mul.214, f32[128]{0:T(128)S(1)} %add_rsqrt_fusion.1), kind=kOutput, calls=%fused_computation.38 | convolution fusion | flops 2149842944 | bytes 18899456 | tf_op jit(solution)/shard_map/dot_general | solution.py:58
  303.7 33.4 %while.20 = (s32[]{:T(128)}, f32[4,512]{1,0:T(4,128)S(1)}, f32[4,512]{1,0:T(4,128)S(1)}, f32[4,512,128]{2,1,0:T(8,128)}, s32[16]{0:T(128)S(1)}, /*index=5*/s32[]...) while((s32[]{:T(128)}, f32[4,512]{1,0:T(4,128)S(1)}, ...), condition=%wide.region_10.11_spmd.clone, body=%wide.region_3.10_spmd.clone.sunk | while | flops 551332864 | bytes 27935672 | solution.py:138
  305.8 6.3 %conditional.3 = ((f32[4,512]{1,0:T(4,128)S(1)}, f32[4,512]{1,0:T(4,128)S(1)}, f32[4,512,128]{2,1,0:T(8,128)})) conditional(s32[]{:T(128)} %convert_element_type.117, (f32[4,512]{1,0:T(4,128)S(1)}, f32[4,512]{1,0:T(4,128)S(1)}, f32[4,512,128]{2,1,0:T(8,128)}) %tuple.77, (s32[512]{0:T(512)S(1)}, s32[128]{0:T(128)S(1)}, s32[]{:T(128)}, ...), branch_computations={%region_6.6_spmd, %region_7.9_spmd} | conditional | flops 551292928 | bytes 27925118 | solution.py:136
  339.0 85.9 %all-gather.14.cloned.1.call-done = bf16[2048,4096]{1,0:T(8,128)(2,1)} async-done(((bf16[2048,256]{1,0:T(8,128)(2,1)}), bf16[2048,4096]{1,0:T(8,128)(2,1)}) %all-gather.14.cloned.1.call-update) | async-done | bytes 16777232 | tf_op jit(solution)/shard_map/all_gather | solution.py:147
  424.9 9.2 %convolution_convert_fusion = bf16[128,4096]{1,0:T(8,128)(2,1)} fusion(bf16[128,2048]{0,1:T(8,128)(2,1)S(1)} %bitcast.47, bf16[2048,4096]{1,0:T(8,128)(2,1)} %all-gather.14.cloned.1.call-done), kind=kOutput, calls=%fused_computation.31 | convolution fusion | flops 2148007936 | bytes 18350080 | tf_op jit(solution)/shard_map/dot_general | solution.py:145
  434.1 18.7 %reduce-scatter.2.cloned.1.call-done = bf16[128,2048]{1,0:T(8,128)(2,1)} async-done(((bf16[128,4096]{1,0:T(8,128)(2,1)}), bf16[128,2048]{1,0:T(8,128)(2,1)}) %reduce-scatter.2.cloned.1.call-update) | async-done | bytes 524304 | tf_op jit(solution)/shard_map/reduce_scatter | solution.py:150
  (173 shorter events, 84.9 us)
Async XLA Ops:
  7.2 26.4 %all-gather.8.cloned.1.call-start = ((), (), s32[]{:S(2)}) async-start(), calls=%async_computation.1 | async-start | bytes 1572864 | tf_op jit(solution)/shard_map/all_gather | solution.py:49
  7.9 102.8 %all-gather.10.cloned.1.call-start = ((), (), s32[]{:S(2)}) async-start(), calls=%async_computation.2 | async-start | bytes 8912896 | tf_op jit(solution)/shard_map/all_gather | solution.py:67
  9.9 241.6 %all-gather.16.cloned.1.call-start = ((), (), s32[]{:S(2)}) async-start(), calls=%async_computation.6 | async-start | bytes 2228224 | tf_op jit(solution)/shard_map/all_gather | solution.py:101
  35.1 82.5 %copy-start.4 = (s32[16]{0:T(128)S(1)}, s32[16]{0:T(128)}, u32[]{:S(2)}) copy-start(s32[16]{0:T(128)} %param.14) | copy-start | bytes 196
  115.7 124.0 %copy-start.5 = (bf16[2048]{0:T(1024)(128)(2,1)S(1)}, bf16[2048]{0:T(1024)(128)(2,1)}, u32[]{:S(2)}) copy-start(bf16[2048]{0:T(1024)(128)(2,1)} %param.17) | copy-start | bytes 12292
  116.4 176.8 %all-gather.12.cloned.1.call-start = ((), (), s32[]{:S(2)}) async-start(), calls=%async_computation.3 | async-start | bytes 17825792 | tf_op jit(solution)/shard_map/all_gather | solution.py:60
  117.0 307.9 %all-gather.14.cloned.1.call-start = ((), (), s32[]{:S(2)}) async-start(), calls=%async_computation.4 | async-start | bytes 17825792 | tf_op jit(solution)/shard_map/all_gather | solution.py:147
  117.6 335.3 %reduce-scatter.2.cloned.1.call-start = ((), (), s32[]{:S(2)}) async-start(), calls=%async_computation.5 | async-start | bytes 1572864 | tf_op jit(solution)/shard_map/reduce_scatter | solution.py:150
  120.0 7.3 %collective-permute-start = (bf16[128,512]{0,1:T(8,128)(2,1)S(1)}, bf16[128,512]{0,1:T(8,128)(2,1)S(1)}, u32[]{:S(2)}, u32[]{:S(2)}) collective-permute-start(bf16[128,512]{0,1:T(8,128)(2,1)S(1)} %bitcast.52), channel_id=1, source_target_pairs={{0,2},{2,4},{4,6},{6,8},{8,10},{10,12},{12,14},{14,16},{16,18},{18... | collective-permute-start | bytes 393224 | tf_op jit(solution)/shard_map/ppermute | solution.py:97
  127.3 8.0 %collective-permute-start.1 = (bf16[128,512]{0,1:T(8,128)(2,1)S(1)}, bf16[128,512]{0,1:T(8,128)(2,1)S(1)}, u32[]{:S(2)}, u32[]{:S(2)}) collective-permute-start(bf16[128,512]{0,1:T(8,128)(2,1)S(1)} %collective-permute-done), channel_id=1, source_target_pairs={{0,2},{2,4},{4,6},{6,8},{8,10},{10,12},{12,14},{14,16},{16,18},{18... | collective-permute-start | bytes 393224 | tf_op jit(solution)/shard_map/ppermute | solution.py:97
  135.2 7.1 %collective-permute-start.2 = (bf16[128,512]{0,1:T(8,128)(2,1)S(1)}, bf16[128,512]{0,1:T(8,128)(2,1)S(1)}, u32[]{:S(2)}, u32[]{:S(2)}) collective-permute-start(bf16[128,512]{0,1:T(8,128)(2,1)S(1)} %collective-permute-done.1), channel_id=1, source_target_pairs={{0,2},{2,4},{4,6},{6,8},{8,10},{10,12},{12,14},{14,16},{16,18},{18... | collective-permute-start | bytes 393224 | tf_op jit(solution)/shard_map/ppermute | solution.py:97
  142.3 8.5 %collective-permute-start.3 = (bf16[128,512]{0,1:T(8,128)(2,1)S(1)}, bf16[128,512]{0,1:T(8,128)(2,1)S(1)}, u32[]{:S(2)}, u32[]{:S(2)}) collective-permute-start(bf16[128,512]{0,1:T(8,128)(2,1)S(1)} %collective-permute-done.2), channel_id=1, source_target_pairs={{0,2},{2,4},{4,6},{6,8},{8,10},{10,12},{12,14},{14,16},{16,18},{18... | collective-permute-start | bytes 393224 | tf_op jit(solution)/shard_map/ppermute | solution.py:97
  150.8 7.3 %collective-permute-start.4 = (bf16[128,512]{0,1:T(8,128)(2,1)S(1)}, bf16[128,512]{0,1:T(8,128)(2,1)S(1)}, u32[]{:S(2)}, u32[]{:S(2)}) collective-permute-start(bf16[128,512]{0,1:T(8,128)(2,1)S(1)} %collective-permute-done.3), channel_id=1, source_target_pairs={{0,2},{2,4},{4,6},{6,8},{8,10},{10,12},{12,14},{14,16},{16,18},{18... | collective-permute-start | bytes 393224 | tf_op jit(solution)/shard_map/ppermute | solution.py:97
  158.1 7.1 %collective-permute-start.5 = (bf16[128,512]{0,1:T(8,128)(2,1)S(1)}, bf16[128,512]{0,1:T(8,128)(2,1)S(1)}, u32[]{:S(2)}, u32[]{:S(2)}) collective-permute-start(bf16[128,512]{0,1:T(8,128)(2,1)S(1)} %collective-permute-done.4), channel_id=1, source_target_pairs={{0,2},{2,4},{4,6},{6,8},{8,10},{10,12},{12,14},{14,16},{16,18},{18... | collective-permute-start | bytes 393224 | tf_op jit(solution)/shard_map/ppermute | solution.py:97
  165.2 7.2 %collective-permute-start.6 = (bf16[128,512]{0,1:T(8,128)(2,1)S(1)}, bf16[128,512]{0,1:T(8,128)(2,1)S(1)}, u32[]{:S(2)}, u32[]{:S(2)}) collective-permute-start(bf16[128,512]{0,1:T(8,128)(2,1)S(1)} %collective-permute-done.5), channel_id=1, source_target_pairs={{0,2},{2,4},{4,6},{6,8},{8,10},{10,12},{12,14},{14,16},{16,18},{18... | collective-permute-start | bytes 393224 | tf_op jit(solution)/shard_map/ppermute | solution.py:97
  172.4 10.0 %collective-permute-start.7 = (bf16[128,512]{0,1:T(8,128)(2,1)S(1)}, bf16[128,512]{0,1:T(8,128)(2,1)S(1)}, u32[]{:S(2)}, u32[]{:S(2)}) collective-permute-start(bf16[128,512]{0,1:T(8,128)(2,1)S(1)} %collective-permute-done.6), channel_id=1, source_target_pairs={{0,2},{2,4},{4,6},{6,8},{8,10},{10,12},{12,14},{14,16},{16,18},{18... | collective-permute-start | bytes 393224 | tf_op jit(solution)/shard_map/ppermute | solution.py:97
  182.4 10.0 %collective-permute-start.8 = (bf16[128,512]{0,1:T(8,128)(2,1)S(1)}, bf16[128,512]{0,1:T(8,128)(2,1)S(1)}, u32[]{:S(2)}, u32[]{:S(2)}) collective-permute-start(bf16[128,512]{0,1:T(8,128)(2,1)S(1)} %collective-permute-done.7), channel_id=1, source_target_pairs={{0,2},{2,4},{4,6},{6,8},{8,10},{10,12},{12,14},{14,16},{16,18},{18... | collective-permute-start | bytes 393224 | tf_op jit(solution)/shard_map/ppermute | solution.py:97
  192.5 10.0 %collective-permute-start.9 = (bf16[128,512]{0,1:T(8,128)(2,1)S(1)}, bf16[128,512]{0,1:T(8,128)(2,1)S(1)}, u32[]{:S(2)}, u32[]{:S(2)}) collective-permute-start(bf16[128,512]{0,1:T(8,128)(2,1)S(1)} %collective-permute-done.8), channel_id=1, source_target_pairs={{0,2},{2,4},{4,6},{6,8},{8,10},{10,12},{12,14},{14,16},{16,18},{18... | collective-permute-start | bytes 393224 | tf_op jit(solution)/shard_map/ppermute | solution.py:97
  202.5 10.0 %collective-permute-start.10 = (bf16[128,512]{0,1:T(8,128)(2,1)S(1)}, bf16[128,512]{0,1:T(8,128)(2,1)S(1)}, u32[]{:S(2)}, u32[]{:S(2)}) collective-permute-start(bf16[128,512]{0,1:T(8,128)(2,1)S(1)} %collective-permute-done.9), channel_id=1, source_target_pairs={{0,2},{2,4},{4,6},{6,8},{8,10},{10,12},{12,14},{14,16},{16,18},{18... | collective-permute-start | bytes 393224 | tf_op jit(solution)/shard_map/ppermute | solution.py:97
  212.5 7.2 %collective-permute-start.11 = (bf16[128,512]{0,1:T(8,128)(2,1)S(1)}, bf16[128,512]{0,1:T(8,128)(2,1)S(1)}, u32[]{:S(2)}, u32[]{:S(2)}) collective-permute-start(bf16[128,512]{0,1:T(8,128)(2,1)S(1)} %collective-permute-done.10), channel_id=1, source_target_pairs={{0,2},{2,4},{4,6},{6,8},{8,10},{10,12},{12,14},{14,16},{16,18},{18... | collective-permute-start | bytes 393224 | tf_op jit(solution)/shard_map/ppermute | solution.py:97
  219.6 10.0 %collective-permute-start.12 = (bf16[128,512]{0,1:T(8,128)(2,1)S(1)}, bf16[128,512]{0,1:T(8,128)(2,1)S(1)}, u32[]{:S(2)}, u32[]{:S(2)}) collective-permute-start(bf16[128,512]{0,1:T(8,128)(2,1)S(1)} %collective-permute-done.11), channel_id=1, source_target_pairs={{0,2},{2,4},{4,6},{6,8},{8,10},{10,12},{12,14},{14,16},{16,18},{18... | collective-permute-start | bytes 393224 | tf_op jit(solution)/shard_map/ppermute | solution.py:97
  229.7 10.0 %collective-permute-start.13 = (bf16[128,512]{0,1:T(8,128)(2,1)S(1)}, bf16[128,512]{0,1:T(8,128)(2,1)S(1)}, u32[]{:S(2)}, u32[]{:S(2)}) collective-permute-start(bf16[128,512]{0,1:T(8,128)(2,1)S(1)} %collective-permute-done.12), channel_id=1, source_target_pairs={{0,2},{2,4},{4,6},{6,8},{8,10},{10,12},{12,14},{14,16},{16,18},{18... | collective-permute-start | bytes 393224 | tf_op jit(solution)/shard_map/ppermute | solution.py:97
  239.7 10.0 %collective-permute-start.14 = (bf16[128,512]{0,1:T(8,128)(2,1)S(1)}, bf16[128,512]{0,1:T(8,128)(2,1)S(1)}, u32[]{:S(2)}, u32[]{:S(2)}) collective-permute-start(bf16[128,512]{0,1:T(8,128)(2,1)S(1)} %collective-permute-done.13), channel_id=1, source_target_pairs={{0,2},{2,4},{4,6},{6,8},{8,10},{10,12},{12,14},{14,16},{16,18},{18... | collective-permute-start | bytes 393224 | tf_op jit(solution)/shard_map/ppermute | solution.py:97
  251.2 42.0 %copy-start = (bf16[128,4096]{1,0:T(8,128)(2,1)S(1)}, bf16[128,4096]{1,0:T(8,128)(2,1)}, u32[]{:S(2)}) copy-start(bf16[128,4096]{1,0:T(8,128)(2,1)} %all-gather.8.cloned.1.call-done) | copy-start | bytes 3145732
  (10 other events, 49.6 us)
Sparse Core Ops, SparseCore 0:
  9.5 23.9 all-gather.7
  36.3 74.2 all-gather.9
  116.5 41.7 all-gather.15
  160.3 132.7 all-gather.11
  295.2 129.6 all-gather.13
  434.2 18.5 reduce-scatter.1
